TPU v7x, 128 devices: a whole 4x4x4 slice. The times are simulated.
128 devices in a mesh: pipe: 2 (over x_lo), tensor: 4 (over x_hi, core), dp: 16 (over z, y).
Axes of the slice: x: 4 (x_hi: 2, x_lo: 2; x = x_hi * 2 + x_lo), y: 4, z: 4, core: 2. Of those that a mesh axis runs over, the one named last changes fastest.
Arguments:
- inputs: bfloat16 [2, 2048, 16384], P(None, 'dp', 'tensor'), may hold values from -6 to 6
- w_in: bfloat16 [2, 16384, 1024], P('pipe', ('tensor', 'dp')), may hold values from -0.046875 to 0.046875
- w_out: bfloat16 [2, 1024, 16384], P('pipe', None, ('tensor', 'dp')), may hold values from -0.1875 to 0.1875
- cotangent: bfloat16 [2, 2048, 16384], P(None, 'dp', 'tensor'), may hold values from -6 to 6
Outputs:
- update_in: float32 [2, 16384, 1024], P('pipe', ('tensor', 'dp'))
- update_out: float32 [2, 1024, 16384], P('pipe', None, ('tensor', 'dp'))
- grad_norm: float32 [], replicated
All inputs are finite; a program needn't handle non-finite values.
Results may differ from a plain program's by a relative error of at most 0.008.
Values may be sent and summed in bfloat16 or wider, within the bound.
No kernel may reach another device: no remote copies, remote signals or barrier semaphores. Data moves between devices by JAX's collectives and lax.ppermute only.
A program may use at most 192 MiB of HBM per device.

v0:
```python
import jax
import jax.numpy as jnp
from jax import lax
from jax.sharding import Mesh
from jax.sharding import PartitionSpec as P

CLIP_NORM = 16384
DP = ("dp_0", "dp_1")
TENSOR = ("tensor_0", "tensor_1")
PIPE_TENSOR_DP = ("pipe", "tensor_0", "tensor_1", "dp_0", "dp_1")
TENSOR_DP = ("tensor_0", "tensor_1", "dp_0", "dp_1")


def rows_first(arrays, axis, dims):
    turned = [jnp.moveaxis(a, dim, 0) for a, dim in zip(arrays, dims)]
    both = jnp.concatenate([t.reshape(len(t), -1) for t in turned], axis=1)
    filled, at, done = (lax.all_gather(both, axis, axis=0, tiled=True), 0, [])
    for t, dim in zip(turned, dims):
        section = filled[:, at : at + t[0].size].reshape(-1, *t.shape[1:])
        done.append(jnp.moveaxis(section, 0, dim))
        at += t[0].size
    return tuple(done)


def total_of_pieces(value, axis):
    return lax.all_gather(value, axis).sum(0)


def from_behind(value, axis, by):
    count = lax.axis_size(axis)
    pairs = [(i, i + by) for i in range(count) if 0 <= i + by < count]
    return lax.ppermute(value, axis, pairs)


def by_axis(value, axes):
    for axis in axes:
        value = lax.psum(value, axis)
    return value


def unit_forward(preact, unused):
    return jax.nn.silu(preact).astype(jnp.bfloat16)


def unit_backward(upward, preact):
    sigmoid_value = jax.nn.sigmoid(preact)
    return (upward * sigmoid_value * (1.0 + preact * (1.0 - sigmoid_value))).astype(jnp.bfloat16)


def kahan_add(running, carried, grad_term):
    corrected = grad_term - carried.astype(jnp.float32)
    summed = (running.astype(jnp.float32) + corrected).astype(jnp.bfloat16)
    carried = (summed.astype(jnp.float32) - running.astype(jnp.float32) - corrected).astype(
        jnp.bfloat16
    )
    return (summed, carried)


def contract_last(first_operand, second_operand):
    return lax.dot_general(
        first_operand, second_operand, (((1,), (1,)), ((), ())), preferred_element_type=jnp.float32
    )


def keep_state(state, x_part, act_part, err_part, slope_part):
    return state


def on_device(inputs, w_in, w_out, cotangent):
    sections = lax.axis_size("pipe")
    section_index = lax.axis_index("pipe")
    micro_count = inputs.shape[0]
    step_count = micro_count + sections - 1
    w_first, w_second = rows_first((w_in[0], w_out[0]), DP, (0, 1))
    section_inputs, section_seeds = (inputs, cotangent)
    groups = 1
    stat_rows = section_inputs.shape[1]

    def combine_units(partial_value, unit_fn, kept_stat):
        whole_sum = total_of_pieces(partial_value, TENSOR)
        return (whole_sum, unit_fn(whole_sum, kept_stat))

    row_count = section_inputs.shape[1]
    col_count = section_inputs.shape[2]
    hidden = w_first.shape[1]
    zero_stat = jnp.zeros((stat_rows, hidden), jnp.float32)
    zero_rows = jnp.zeros((row_count, col_count), jnp.bfloat16)
    zero_units = jnp.zeros((row_count, hidden), jnp.float32)

    def project_in(current):
        return jnp.dot(current, w_first, preferred_element_type=jnp.float32)

    def project_back(current):
        return contract_last(current, w_second)

    def no_units(current):
        return zero_units

    def residual_forward(current, activation):
        return (
            current.astype(jnp.float32)
            + jnp.dot(activation, w_second, preferred_element_type=jnp.float32)
        ).astype(jnp.bfloat16)

    def residual_backward(current, slope):
        return (current.astype(jnp.float32) + contract_last(slope, w_first)).astype(jnp.bfloat16)

    def no_rows(current, other):
        return zero_rows

    def forward_step(state_carry, step_index):
        incoming, kept_x, kept_pre, kept_act = state_carry
        micro_index = step_index - section_index
        active = jnp.logical_and(micro_index >= 0, micro_index < micro_count)
        micro_slot = jnp.clip(micro_index, 0, micro_count - 1)
        own_rows = lax.dynamic_index_in_dim(section_inputs, micro_slot, 0, False)
        current = jnp.where(section_index == 0, own_rows, incoming)
        partial_value = lax.cond(active, project_in, no_units, current)
        preact, activation = combine_units(partial_value, unit_forward, zero_stat)
        result = lax.cond(active, residual_forward, no_rows, current, activation)
        kept_x = jnp.where(
            active, lax.dynamic_update_index_in_dim(kept_x, current, micro_slot, 0), kept_x
        )
        kept_pre = jnp.where(
            active, lax.dynamic_update_index_in_dim(kept_pre, preact, micro_slot, 0), kept_pre
        )
        kept_act = jnp.where(
            active, lax.dynamic_update_index_in_dim(kept_act, activation, micro_slot, 0), kept_act
        )
        outgoing = from_behind(result, "pipe", 1)
        return ((outgoing, kept_x, kept_pre, kept_act), None)

    forward_init = (
        zero_rows,
        jnp.zeros((micro_count, row_count, col_count), jnp.bfloat16),
        jnp.zeros((micro_count, stat_rows, hidden), jnp.float32),
        jnp.zeros((micro_count, row_count, hidden), jnp.bfloat16),
    )
    forward_final, unused_out = lax.scan(forward_step, forward_init, jnp.arange(step_count))
    unused_rows, kept_x, kept_pre, kept_act = forward_final

    def accumulate(state, x_part, act_part, err_part, slope_part):
        sum_in, err_in, sum_out, err_out = state
        x_groups = x_part.reshape(groups, -1, col_count)
        slope_groups = slope_part.reshape(groups, -1, hidden)
        act_groups = act_part.reshape(groups, -1, hidden)
        err_groups = err_part.reshape(groups, -1, col_count)
        grad_in = jnp.einsum(
            "gtc,gth->gch", x_groups, slope_groups, preferred_element_type=jnp.float32
        )
        grad_out = jnp.einsum(
            "gth,gtc->ghc", act_groups, err_groups, preferred_element_type=jnp.float32
        )
        sum_in, err_in = kahan_add(sum_in, err_in, grad_in)
        sum_out, err_out = kahan_add(sum_out, err_out, grad_out)
        return (sum_in, err_in, sum_out, err_out)

    def backward_step(state_carry, step_index):
        incoming, sums = state_carry
        micro_index = step_index - (sections - 1 - section_index)
        active = jnp.logical_and(micro_index >= 0, micro_index < micro_count)
        micro_slot = jnp.clip(micro_index, 0, micro_count - 1)
        own_rows = lax.dynamic_index_in_dim(section_seeds, micro_slot, 0, False)
        current = jnp.where(section_index == sections - 1, own_rows, incoming)
        partial_value = lax.cond(active, project_back, no_units, current)
        preact = lax.dynamic_index_in_dim(kept_pre, micro_slot, 0, False)
        unused_stat, slope = combine_units(partial_value, unit_backward, preact)
        x_here = lax.dynamic_index_in_dim(kept_x, micro_slot, 0, False)
        act_here = lax.dynamic_index_in_dim(kept_act, micro_slot, 0, False)
        sums = lax.cond(active, accumulate, keep_state, sums, x_here, act_here, current, slope)
        result = lax.cond(active, residual_backward, no_rows, current, slope)
        outgoing = from_behind(result, "pipe", -1)
        return ((outgoing, sums), None)

    sums_init = (
        jnp.zeros((groups, col_count, hidden), jnp.bfloat16),
        jnp.zeros((groups, col_count, hidden), jnp.bfloat16),
        jnp.zeros((groups, hidden, col_count), jnp.bfloat16),
        jnp.zeros((groups, hidden, col_count), jnp.bfloat16),
    )
    backward_final, unused_back = lax.scan(
        backward_step, (zero_rows, sums_init), jnp.arange(step_count)
    )
    unused_errors, final_sums = backward_final
    sum_in, err_in, sum_out, err_out = final_sums
    total_in = jnp.sum(sum_in.astype(jnp.float32) - err_in.astype(jnp.float32), axis=0)
    total_out = jnp.sum(sum_out.astype(jnp.float32) - err_out.astype(jnp.float32), axis=0)
    total_in, total_out = (
        lax.psum_scatter(total_in, DP, scatter_dimension=0, tiled=True),
        lax.psum_scatter(total_out, DP, scatter_dimension=1, tiled=True),
    )
    squares = jnp.sum(total_in * total_in) + jnp.sum(total_out * total_out)
    norm_squared = by_axis(squares, PIPE_TENSOR_DP)
    grad_norm = jnp.sqrt(norm_squared)
    factor = jnp.minimum(1.0, CLIP_NORM / grad_norm)
    return ((total_in * factor)[None], (total_out * factor)[None], grad_norm)


def solution(mesh):
    split = Mesh(
        mesh.devices.reshape(mesh.shape["pipe"], 2, 2, 4, 4),
        ("pipe", "tensor_0", "tensor_1", "dp_0", "dp_1"),
    )
    placed = (
        P(None, DP, TENSOR),
        P("pipe", TENSOR_DP, None),
        P("pipe", None, TENSOR_DP),
        P(None, DP, TENSOR),
    )
    return jax.shard_map(
        on_device,
        mesh=split,
        in_specs=placed,
        out_specs=(P("pipe", TENSOR_DP, None), P("pipe", None, TENSOR_DP), P()),
        check_vma=False,
    )
```

profile of v0, /device:TPU:0, one launch (start us, length us, event | category | flops | bytes accessed | tf_op | source)
XLA Modules:
  0.0 888.3 jit_solution(17027753523874269229)
XLA Ops:
  10.6 114.0 %all-gather.10.cloned.1.call-done = bf16[4096,2048]{1,0:T(8,128)(2,1)} async-done(((bf16[256,2048]{1,0:T(8,128)(2,1)}), bf16[4096,2048]{1,0:T(8,128)(2,1)}) %all-gather.10.cloned.1.call-update) | async-done | bytes 16777232 | tf_op jit(solution)/shard_map/all_gather | solution.py:17
  124.6 11.7 %fusion.32 = (bf16[4096,1024]{1,0:T(8,128)(2,1)}, bf16[1024,4096]{0,1:T(8,128)(2,1)}) fusion(bf16[4096,2048]{1,0:T(8,128)(2,1)} %all-gather.10.cloned.1.call-done), kind=kLoop, calls=%fused_computation.55 | loop fusion | bytes 33554432 | tf_op jit(solution)/shard_map/slice | solution.py:19
  136.3 11.3 %copy.9 = bf16[1024,4096]{1,0:T(8,128)(2,1)} copy(bf16[1024,4096]{0,1:T(8,128)(2,1)} %get-tuple-element.500) | data formatting | bytes 16777216 | tf_op jit(solution)/shard_map/while | solution.py:181
  150.4 213.6 %while.37 = (s32[]{:T(128)}, bf16[128,4096]{1,0:T(8,128)(2,1)}, bf16[2,128,4096]{2,1,0:T(8,128)(2,1)}, f32[2,128,1024]{2,1,0:T(8,128)S(1)}, bf16[2,128,1024]{2,1...) while((s32[]{:T(128)}, bf16[128,4096]{1,0:T(8,128)(2,1)}, ...), condition=%wide.region_6.7_spmd, body=%wide.region_0.6_spmd.sunk | while | flops 2152071168 | bytes 50332584 | solution.py:139
  154.9 4.6 conditional.10
  154.9 4.6 fusion.33
  160.3 26.3 %all-gather.12.cloned.1.call-done = f32[512,1024]{1,0:T(8,128)} async-done(((f32[128,1024]{1,0:T(8,128)}), f32[512,1024]{1,0:T(8,128)}) %all-gather.12.cloned.1.call-update) | async-done | bytes 2097168 | tf_op jit(solution)/shard_map/while/body/eval_jaxpr/all_gather | solution.py:26
  188.6 5.6 conditional.11
  188.6 5.6 fusion
  195.9 23.0 %collective-permute-done = bf16[128,4096]{1,0:T(8,128)(2,1)S(1)} collective-permute-done((bf16[128,4096]{1,0:T(8,128)(2,1)}, bf16[128,4096]{1,0:T(8,128)(2,1)S(1)}, u32[]{:S(2)}, u32[]{:S(2)}) %collective-permute-start) | collective-permute-done | bytes 1048608 | tf_op jit(solution)/shard_map/while/body/eval_jaxpr/ppermute | solution.py:32
  224.4 4.6 conditional.10
  224.4 4.6 fusion.33
  229.8 27.7 %all-gather.12.cloned.1.call-done = f32[512,1024]{1,0:T(8,128)} async-done(((f32[128,1024]{1,0:T(8,128)}), f32[512,1024]{1,0:T(8,128)}) %all-gather.12.cloned.1.call-update) | async-done | bytes 2097168 | tf_op jit(solution)/shard_map/while/body/eval_jaxpr/all_gather | solution.py:26
  259.5 5.6 conditional.11
  259.5 5.6 fusion
  267.9 22.8 %collective-permute-done = bf16[128,4096]{1,0:T(8,128)(2,1)S(1)} collective-permute-done((bf16[128,4096]{1,0:T(8,128)(2,1)}, bf16[128,4096]{1,0:T(8,128)(2,1)S(1)}, u32[]{:S(2)}, u32[]{:S(2)}) %collective-permute-start) | collective-permute-done | bytes 1048608 | tf_op jit(solution)/shard_map/while/body/eval_jaxpr/ppermute | solution.py:32
  297.0 32.9 %all-gather.12.cloned.1.call-done = f32[512,1024]{1,0:T(8,128)} async-done(((f32[128,1024]{1,0:T(8,128)}), f32[512,1024]{1,0:T(8,128)}) %all-gather.12.cloned.1.call-update) | async-done | bytes 2097168 | tf_op jit(solution)/shard_map/while/body/eval_jaxpr/all_gather | solution.py:26
  332.9 7.1 collective-permute-start
  340.3 22.8 %collective-permute-done = bf16[128,4096]{1,0:T(8,128)(2,1)S(1)} collective-permute-done((bf16[128,4096]{1,0:T(8,128)(2,1)}, bf16[128,4096]{1,0:T(8,128)(2,1)S(1)}, u32[]{:S(2)}, u32[]{:S(2)}) %collective-permute-start) | collective-permute-done | bytes 1048608 | tf_op jit(solution)/shard_map/while/body/eval_jaxpr/ppermute | solution.py:32
  364.0 4.4 broadcast.38
  372.8 4.4 broadcast.39
  381.7 218.9 %while.38 = (s32[]{:T(128)}, bf16[128,4096]{1,0:T(8,128)(2,1)S(1)}, bf16[1,4096,1024]{2,1,0:T(8,128)(2,1)}, bf16[1,4096,1024]{2,1,0:T(8,128)(2,1)}, bf16[1,1024,...) while((s32[]{:T(128)}, bf16[128,4096]{1,0:T(8,128)(2,1)S(1)}, ...), condition=%wide.region_15.16_spmd, body=%wide.region_7.15_spmd.sunk | while | flops 4374134784 | bytes 187172016 | solution.py:181
  385.4 34.3 %all-gather.14.cloned.1.call-done = f32[512,1024]{1,0:T(8,128)} async-done(((f32[128,1024]{1,0:T(8,128)}), f32[512,1024]{1,0:T(8,128)}) %all-gather.14.cloned.1.call-update) | async-done | bytes 2097168 | tf_op jit(solution)/shard_map/while/body/eval_jaxpr/all_gather | solution.py:26
  424.1 30.4 %collective-permute-done.1 = bf16[128,4096]{1,0:T(8,128)(2,1)S(1)} collective-permute-done((bf16[128,4096]{1,0:T(8,128)(2,1)}, bf16[128,4096]{1,0:T(8,128)(2,1)S(1)}, u32[]{:S(2)}, u32[]{:S(2)}) %collective-permute-start.1) | collective-permute-done | bytes 1048608 | tf_op jit(solution)/shard_map/while/body/eval_jaxpr/ppermute | solution.py:32
  457.2 6.4 conditional.12
  457.2 6.3 fusion.34
  464.3 27.5 %all-gather.14.cloned.1.call-done = f32[512,1024]{1,0:T(8,128)} async-done(((f32[128,1024]{1,0:T(8,128)}), f32[512,1024]{1,0:T(8,128)}) %all-gather.14.cloned.1.call-update) | async-done | bytes 2097168 | tf_op jit(solution)/shard_map/while/body/eval_jaxpr/all_gather | solution.py:26
  493.9 6.3 conditional.13
  493.9 6.2 fusion.9
  502.4 25.6 %conditional.14 = ((bf16[1,4096,1024]{2,1,0:T(8,128)(2,1)}, bf16[1,4096,1024]{2,1,0:T(8,128)(2,1)}, bf16[1,1024,4096]{2,1,0:T(8,128)(2,1)}, bf16[1,1024,4096]{2,1,0:T(8,128)(2,1)})) conditional(s32[]{:T(128)} %convert_element_type.173, (bf16[1,4096,1024]{2,1,0:T(8,128)(2,1)}, bf16[1,4096,1024]{2,1,0:T(8,128)(2,1)}, ...), branch_computations={%region_13.13_spmd, %region_14.14_spmd} | conditional | flops 2222981120 | bytes 136839776 | solution.py:170
  502.5 12.9 %fusion.12 = (bf16[1,4096,1024]{2,1,0:T(8,128)(2,1)}, bf16[1,4096,1024]{2,1,0:T(8,128)(2,1)}) fusion(bf16[1,4096,1024]{2,1,0:T(8,128)(2,1)} %get-tuple-element.369, bf16[1,4096,1024]{2,1,0:T(8,128)(2,1)} %get-tuple-element.373, bf16[128,1024]{1,0:T(8,128)(2,1)S(1)} %get-tuple-element.372, bf16[2,128,4096]{2,1,0:T(8,128)(2,1)} %get-tuple-element.370, ...), kind=kOutput, calls=%fused_computation.24 | convolution fusion | flops 1111490560 | bytes 34865664 | tf_op jit(solution)/shard_map/while/body/eval_jaxpr/cond/branch_1_fun/gtc,gth->gch/dot_general | solution.py:148
  515.4 9.3 %fusion.15 = (bf16[1,1024,4096]{2,1,0:T(8,128)(2,1)}, bf16[1,1024,4096]{2,1,0:T(8,128)(2,1)S(1)}) fusion(bf16[1,1024,4096]{2,1,0:T(8,128)(2,1)S(1)} %copy-done, bf16[1,1024,4096]{2,1,0:T(8,128)(2,1)} %get-tuple-element.377, bf16[128,4096]{1,0:T(8,128)(2,1)S(1)} %get-tuple-element.376, bf16[2,128,1024]{2,1,0:T(8,128)(2,1)S(1)} %get-tuple-element.375, ...), kind=kOutput, calls=%fused_computation.27 | convolution fusion | flops 1111490560 | bytes 34865156 | tf_op jit(solution)/shard_map/while/body/eval_jaxpr/cond/branch_1_fun/gth,gtc->ghc/dot_general | solution.py:151
  531.1 6.4 conditional.12
  531.2 6.3 fusion.34
  538.3 25.6 %all-gather.14.cloned.1.call-done = f32[512,1024]{1,0:T(8,128)} async-done(((f32[128,1024]{1,0:T(8,128)}), f32[512,1024]{1,0:T(8,128)}) %all-gather.14.cloned.1.call-update) | async-done | bytes 2097168 | tf_op jit(solution)/shard_map/while/body/eval_jaxpr/all_gather | solution.py:26
  565.9 6.3 conditional.13
  566.0 6.3 fusion.9
  574.5 25.6 %conditional.14 = ((bf16[1,4096,1024]{2,1,0:T(8,128)(2,1)}, bf16[1,4096,1024]{2,1,0:T(8,128)(2,1)}, bf16[1,1024,4096]{2,1,0:T(8,128)(2,1)}, bf16[1,1024,4096]{2,1,0:T(8,128)(2,1)})) conditional(s32[]{:T(128)} %convert_element_type.173, (bf16[1,4096,1024]{2,1,0:T(8,128)(2,1)}, bf16[1,4096,1024]{2,1,0:T(8,128)(2,1)}, ...), branch_computations={%region_13.13_spmd, %region_14.14_spmd} | conditional | flops 2222981120 | bytes 136839776 | solution.py:170
  574.5 12.9 %fusion.12 = (bf16[1,4096,1024]{2,1,0:T(8,128)(2,1)}, bf16[1,4096,1024]{2,1,0:T(8,128)(2,1)}) fusion(bf16[1,4096,1024]{2,1,0:T(8,128)(2,1)} %get-tuple-element.369, bf16[1,4096,1024]{2,1,0:T(8,128)(2,1)} %get-tuple-element.373, bf16[128,1024]{1,0:T(8,128)(2,1)S(1)} %get-tuple-element.372, bf16[2,128,4096]{2,1,0:T(8,128)(2,1)} %get-tuple-element.370, ...), kind=kOutput, calls=%fused_computation.24 | convolution fusion | flops 1111490560 | bytes 34865664 | tf_op jit(solution)/shard_map/while/body/eval_jaxpr/cond/branch_1_fun/gtc,gth->gch/dot_general | solution.py:148
  587.4 9.3 %fusion.15 = (bf16[1,1024,4096]{2,1,0:T(8,128)(2,1)}, bf16[1,1024,4096]{2,1,0:T(8,128)(2,1)S(1)}) fusion(bf16[1,1024,4096]{2,1,0:T(8,128)(2,1)S(1)} %copy-done, bf16[1,1024,4096]{2,1,0:T(8,128)(2,1)} %get-tuple-element.377, bf16[128,4096]{1,0:T(8,128)(2,1)S(1)} %get-tuple-element.376, bf16[2,128,1024]{2,1,0:T(8,128)(2,1)S(1)} %get-tuple-element.375, ...), kind=kOutput, calls=%fused_computation.27 | convolution fusion | flops 1111490560 | bytes 34865156 | tf_op jit(solution)/shard_map/while/body/eval_jaxpr/cond/branch_1_fun/gth,gtc->ghc/dot_general | solution.py:151
  600.6 12.2 %subtract_bitcast_fusion = f32[1024,4096]{1,0:T(8,128)} fusion(bf16[1,1024,4096]{2,1,0:T(8,128)(2,1)} %get-tuple-element.414, bf16[1,1024,4096]{2,1,0:T(8,128)(2,1)} %get-tuple-element.413), kind=kLoop, calls=%fused_computation.47 | loop fusion | flops 12582912 | bytes 33554432 | tf_op jit(solution)/shard_map/reduce_sum | solution.py:187
  612.8 13.3 %subtract_bitcast_fusion.1 = f32[4096,1024]{1,0:T(8,128)} fusion(bf16[1,4096,1024]{2,1,0:T(8,128)(2,1)} %get-tuple-element.412, bf16[1,4096,1024]{2,1,0:T(8,128)(2,1)} %get-tuple-element.411), kind=kLoop, calls=%fused_computation.48 | loop fusion | flops 12582912 | bytes 33554432 | tf_op jit(solution)/shard_map/reduce_sum | solution.py:186
  626.1 96.8 %reduce-scatter.5.cloned.1.call-done = f32[1024,256]{1,0:T(8,128)} async-done(((f32[1024,4096]{1,0:T(8,128)}), f32[1024,256]{1,0:T(8,128)}) %reduce-scatter.5.cloned.1.call-update) | async-done | bytes 1048592 | tf_op jit(solution)/shard_map/reduce_scatter | solution.py:190
  725.0 111.5 %reduce-scatter.3.cloned.1.call-done = f32[256,1024]{1,0:T(8,128)} async-done(((f32[4096,1024]{1,0:T(8,128)}), f32[256,1024]{1,0:T(8,128)}) %reduce-scatter.3.cloned.1.call-update) | async-done | bytes 1048592 | tf_op jit(solution)/shard_map/reduce_scatter | solution.py:189
  839.8 5.4 psum.35
  845.3 7.0 psum.36
  855.4 10.5 %psum.38 = f32[]{:T(128)} all-reduce(f32[]{:T(128)} %psum.37), channel_id=1, replica_groups=mesh['pipe'=2,'tensor_0'=2,'tensor_1'=2,'dp_0'=4,'dp_1'=4] {'dp_0'}, use_global_device_ids=true, to_apply=%region_23.24 | all-reduce | flops 1 | bytes 8 | tf_op jit(solution)/shard_map/psum | solution.py:37
  865.9 9.4 %psum.39 = f32[]{:T(128)} all-reduce(f32[]{:T(128)} %psum.38), channel_id=1, replica_groups=mesh['pipe'=2,'tensor_0'=2,'tensor_1'=2,'dp_0'=4,'dp_1'=4] {'dp_1'}, use_global_device_ids=true, to_apply=%region_24.25 | all-reduce | flops 1 | bytes 8 | tf_op jit(solution)/shard_map/psum | solution.py:37
  (120 shorter events, 85.5 us)
Async XLA Ops:
  7.2 117.4 %all-gather.10.cloned.1.call-start = ((), (), s32[]{:S(2)}) async-start(), calls=%async_computation.2 | async-start | bytes 17825792 | tf_op jit(solution)/shard_map/all_gather | solution.py:17
  150.4 36.2 %all-gather.12.cloned.1.call-start = ((), (), s32[]{:S(2)}) async-start(), calls=%async_computation.5 | async-start | bytes 2621440 | tf_op jit(solution)/shard_map/while/body/eval_jaxpr/all_gather | solution.py:26
  159.5 0.8 copy-start.2
  194.3 24.7 %collective-permute-start = (bf16[128,4096]{1,0:T(8,128)(2,1)}, bf16[128,4096]{1,0:T(8,128)(2,1)S(1)}, u32[]{:S(2)}, u32[]{:S(2)}) collective-permute-start(bf16[128,4096]{1,0:T(8,128)(2,1)} %get-tuple-element.782), channel_id=1, source_target_pairs={{0,64},{1,65},{2,66},{3,67},{4,68},{5,69},{6,70},{7,71},{8,72},{9,... | collective-permute-start | bytes 3145736 | tf_op jit(solution)/shard_map/while/body/eval_jaxpr/ppermute | solution.py:32
  218.9 1.0 copy-start.6
  219.9 37.6 %all-gather.12.cloned.1.call-start = ((), (), s32[]{:S(2)}) async-start(), calls=%async_computation.5 | async-start | bytes 2621440 | tf_op jit(solution)/shard_map/while/body/eval_jaxpr/all_gather | solution.py:26
  229.0 0.8 copy-start.2
  265.1 25.6 %collective-permute-start = (bf16[128,4096]{1,0:T(8,128)(2,1)}, bf16[128,4096]{1,0:T(8,128)(2,1)S(1)}, u32[]{:S(2)}, u32[]{:S(2)}) collective-permute-start(bf16[128,4096]{1,0:T(8,128)(2,1)} %get-tuple-element.782), channel_id=1, source_target_pairs={{0,64},{1,65},{2,66},{3,67},{4,68},{5,69},{6,70},{7,71},{8,72},{9,... | collective-permute-start | bytes 3145736 | tf_op jit(solution)/shard_map/while/body/eval_jaxpr/ppermute | solution.py:32
  290.7 1.0 copy-start.6
  291.7 38.2 %all-gather.12.cloned.1.call-start = ((), (), s32[]{:S(2)}) async-start(), calls=%async_computation.5 | async-start | bytes 2621440 | tf_op jit(solution)/shard_map/while/body/eval_jaxpr/all_gather | solution.py:26
  296.2 0.8 copy-start.2
  332.9 30.1 %collective-permute-start = (bf16[128,4096]{1,0:T(8,128)(2,1)}, bf16[128,4096]{1,0:T(8,128)(2,1)S(1)}, u32[]{:S(2)}, u32[]{:S(2)}) collective-permute-start(bf16[128,4096]{1,0:T(8,128)(2,1)} %get-tuple-element.782), channel_id=1, source_target_pairs={{0,64},{1,65},{2,66},{3,67},{4,68},{5,69},{6,70},{7,71},{8,72},{9,... | collective-permute-start | bytes 3145736 | tf_op jit(solution)/shard_map/while/body/eval_jaxpr/ppermute | solution.py:32
  363.0 1.0 copy-start.6
  364.0 8.8 copy-start.4
  381.8 37.8 %all-gather.14.cloned.1.call-start = ((), (), s32[]{:S(2)}) async-start(), calls=%async_computation.6 | async-start | bytes 2621440 | tf_op jit(solution)/shard_map/while/body/eval_jaxpr/all_gather | solution.py:26
  384.5 37.0 %copy-start.5 = (f32[2,128,1024]{2,1,0:T(8,128)S(1)}, f32[2,128,1024]{2,1,0:T(8,128)}, u32[]{:S(2)}) copy-start(f32[2,128,1024]{2,1,0:T(8,128)} %get-tuple-element.773) | copy-start | bytes 3145732 | tf_op jit(solution)/shard_map/while
  384.6 0.8 copy-start.3
  421.8 1.0 copy-start.7
  422.8 31.7 %collective-permute-start.1 = (bf16[128,4096]{1,0:T(8,128)(2,1)}, bf16[128,4096]{1,0:T(8,128)(2,1)S(1)}, u32[]{:S(2)}, u32[]{:S(2)}) collective-permute-start(bf16[128,4096]{1,0:T(8,128)(2,1)} %copy-done.7), channel_id=1, source_target_pairs={{64,0},{65,1},{66,2},{67,3},{68,4},{69,5},{70,6},{71,7},{72,8},{73... | collective-permute-start | bytes 3145736 | tf_op jit(solution)/shard_map/while/body/eval_jaxpr/ppermute | solution.py:32
  454.6 37.3 %all-gather.14.cloned.1.call-start = ((), (), s32[]{:S(2)}) async-start(), calls=%async_computation.6 | async-start | bytes 2621440 | tf_op jit(solution)/shard_map/while/body/eval_jaxpr/all_gather | solution.py:26
  457.1 36.5 %copy-start.5 = (f32[2,128,1024]{2,1,0:T(8,128)S(1)}, f32[2,128,1024]{2,1,0:T(8,128)}, u32[]{:S(2)}) copy-start(f32[2,128,1024]{2,1,0:T(8,128)} %get-tuple-element.773) | copy-start | bytes 3145732 | tf_op jit(solution)/shard_map/while
  463.5 0.8 copy-start.3
  500.2 1.0 copy-start.7
  501.2 27.4 %collective-permute-start.1 = (bf16[128,4096]{1,0:T(8,128)(2,1)}, bf16[128,4096]{1,0:T(8,128)(2,1)S(1)}, u32[]{:S(2)}, u32[]{:S(2)}) collective-permute-start(bf16[128,4096]{1,0:T(8,128)(2,1)} %copy-done.7), channel_id=1, source_target_pairs={{64,0},{65,1},{66,2},{67,3},{68,4},{69,5},{70,6},{71,7},{72,8},{73... | collective-permute-start | bytes 3145736 | tf_op jit(solution)/shard_map/while/body/eval_jaxpr/ppermute | solution.py:32
  502.5 12.9 %copy-start = (bf16[1,1024,4096]{2,1,0:T(8,128)(2,1)S(1)}, bf16[1,1024,4096]{2,1,0:T(8,128)(2,1)}, u32[]{:S(2)}) copy-start(bf16[1,1024,4096]{2,1,0:T(8,128)(2,1)} %get-tuple-element.374) | copy-start | bytes 25165828 | tf_op jit(solution)/shard_map/while/body/eval_jaxpr/cond
  524.7 3.4 copy-start.1
  528.5 35.4 %all-gather.14.cloned.1.call-start = ((), (), s32[]{:S(2)}) async-start(), calls=%async_computation.6 | async-start | bytes 2621440 | tf_op jit(solution)/shard_map/while/body/eval_jaxpr/all_gather | solution.py:26
  531.1 34.6 %copy-start.5 = (f32[2,128,1024]{2,1,0:T(8,128)S(1)}, f32[2,128,1024]{2,1,0:T(8,128)}, u32[]{:S(2)}) copy-start(f32[2,128,1024]{2,1,0:T(8,128)} %get-tuple-element.773) | copy-start | bytes 3145732 | tf_op jit(solution)/shard_map/while
  537.5 0.8 copy-start.3
  572.2 1.0 copy-start.7
  573.2 27.4 %collective-permute-start.1 = (bf16[128,4096]{1,0:T(8,128)(2,1)}, bf16[128,4096]{1,0:T(8,128)(2,1)S(1)}, u32[]{:S(2)}, u32[]{:S(2)}) collective-permute-start(bf16[128,4096]{1,0:T(8,128)(2,1)} %copy-done.7), channel_id=1, source_target_pairs={{64,0},{65,1},{66,2},{67,3},{68,4},{69,5},{70,6},{71,7},{72,8},{73... | collective-permute-start | bytes 3145736 | tf_op jit(solution)/shard_map/while/body/eval_jaxpr/ppermute | solution.py:32
  574.5 12.9 %copy-start = (bf16[1,1024,4096]{2,1,0:T(8,128)(2,1)S(1)}, bf16[1,1024,4096]{2,1,0:T(8,128)(2,1)}, u32[]{:S(2)}) copy-start(bf16[1,1024,4096]{2,1,0:T(8,128)(2,1)} %get-tuple-element.374) | copy-start | bytes 25165828 | tf_op jit(solution)/shard_map/while/body/eval_jaxpr/cond
  596.7 3.4 copy-start.1
  600.6 122.3 %reduce-scatter.5.cloned.1.call-start = ((), (), s32[]{:S(2)}) async-start(), calls=%async_computation.4 | async-start | bytes 17825792 | tf_op jit(solution)/shard_map/reduce_scatter | solution.py:190
  612.8 223.7 %reduce-scatter.3.cloned.1.call-start = ((), (), s32[]{:S(2)}) async-start(), calls=%async_computation.3 | async-start | bytes 17825792 | tf_op jit(solution)/shard_map/reduce_scatter | solution.py:189
Sparse Core Ops, SparseCore 0:
  10.7 113.8 all-gather.9
  160.5 26.1 all-gather.11
  229.9 27.5 all-gather.11
  297.1 32.7 all-gather.11
  385.5 34.1 all-gather.13
  464.5 27.3 all-gather.13
  538.4 25.4 all-gather.13
  612.9 109.9 reduce-scatter.4
  726.3 110.0 reduce-scatter.2
where the time goes:
time: 890 us; the launch traced here: 888 us
  waiting for transfers between devices  597 us (67%)
  matrix products  90.1 us (10%)
  local copies, waits for them, and re-layouts  66.9 us (8%)
  other arithmetic  62.4 us (7%)
  blocking collectives  35.5 us (4%)
  between operations  17 us (2%)
  starting transfers between devices  15 us (2%)
    all_gather x6, waiting for transfers between devices, total_of_pieces(): return lax.all_gather(value, axis).sum(0)  174 us
    all_gather x1, waiting for transfers between devices, rows_first(): filled, at, done = (lax.all_gather(both, axis, axis=0, tiled=True), 0, [])  114 us
    reduce_scatter x1, waiting for transfers between devices, on_device(): lax.psum_scatter(total_in, DP, scatter_dimension=0, tiled=True)  111 us
    ppermute x6, waiting for transfers between devices, from_behind(): return lax.ppermute(value, axis, pairs)  100 us
    reduce_scatter x1, waiting for transfers between devices, on_device(): lax.psum_scatter(total_out, DP, scatter_dimension=1, tiled=True)  96.8 us
    psum x5, blocking collectives, by_axis(): value = lax.psum(value, axis)  35.5 us
    dot_general x2, matrix products, accumulate(): jnp.einsum('gtc,gth->gch', x_groups, slope_groups, preferred_element_type...  25.8 us
    dot_general x4, matrix products, contract_last(): lax.dot_general(first_operand, second_operand, (((1,), (1,)), ((), ())),...  25.2 us
  transfers between devices with their start and end apart: 15, of which 15 were waited for; matrix products, arithmetic and copies ran while one was open for 7% of the time, Pallas kernels for 0%

commit v1 on v0

v1 whole, which is shorter than its diff:
```python
import jax
import jax.numpy as jnp
from jax import lax
from jax.sharding import Mesh
from jax.sharding import PartitionSpec as P

CLIP_NORM = 16384
AXES = ("p", "h", "c", "z", "y")
BF = jnp.bfloat16
F32 = jnp.float32


def dot(a, b):
    return jnp.dot(a, b, preferred_element_type=F32)


def dot_t0(a, b):
    return lax.dot_general(a, b, (((0,), (0,)), ((), ())), preferred_element_type=F32)


def dot_t1(a, b):
    return lax.dot_general(a, b, (((1,), (1,)), ((), ())), preferred_element_type=F32)


def a2a(value, axes):
    return lax.all_to_all(value, axes, 0, 0, tiled=True)


def silu_bf(pre):
    return jax.nn.silu(pre).astype(BF)


def slope_bf(up, pre):
    s = jax.nn.sigmoid(pre)
    return (up * s * (1.0 + pre * (1.0 - s))).astype(BF)


def on_device(inputs, w_in, w_out, cotangent):
    first = lax.axis_index("p") == 0
    z_index = lax.axis_index("z")
    n_micro, rows, cols = inputs.shape
    tok = n_micro * rows
    hidden = w_in.shape[2]
    own = w_in.shape[1]
    nz, ny, nc = lax.axis_size("z"), lax.axis_size("y"), lax.axis_size("c")
    n_ph = lax.axis_size("p") * lax.axis_size("h")
    half = tok // nc
    mine = half // n_ph
    wide = own * nz

    w_i = w_in[0]
    w_o = w_out[0].T
    w_u = jnp.where(first, w_o, w_i)
    w_v = jnp.where(first, w_i, w_o)
    w_3 = lax.ppermute(w_u, "p", [(0, 1), (1, 0)])
    w_u = lax.all_gather(w_u, "z", axis=0, tiled=True)
    w_v = lax.all_gather(w_v, "y", axis=0, tiled=True)
    w_3 = lax.all_gather(w_3, "z", axis=0, tiled=True)

    x = inputs.reshape(tok, nz, ny, own)
    ct = cotangent.reshape(tok, nz, ny, own)
    u = jnp.where(first, ct, x).transpose(2, 0, 1, 3).reshape(ny * tok, wide)
    v = jnp.where(first, x, ct).transpose(1, 0, 2, 3).reshape(nz * tok, ny * own)
    u = a2a(u, "y")
    v = a2a(v, "z")

    left = jnp.where(first, w_u, w_3)
    right = jnp.where(first, w_3, w_u)
    block = hidden // nz
    left = lax.dynamic_slice_in_dim(left, z_index * block, block, 1)
    m_part = a2a(dot_t0(left, right).astype(BF), ("y", "h", "c"))
    m_rows = m_part.reshape(-1, block // (ny * 4), hidden).astype(F32).sum(0).astype(BF)
    m_rows = lax.all_gather(m_rows, ("h", "c"), axis=0, tiled=True)
    m_all = lax.all_gather(m_rows, ("z", "y"), axis=0, tiled=True)

    a_u = dot(u, w_u).astype(BF).reshape(ny, nc, half, hidden).transpose(1, 0, 2, 3)
    a_v = dot(v, w_v).astype(BF).reshape(nz, nc, half, hidden).transpose(1, 0, 2, 3)
    a_u, a_v = a2a(a_u, "c"), a2a(a_v, "c")
    a_u = a_u.astype(F32).sum(0).astype(BF)
    a_v = a_v.astype(F32).sum(0).astype(BF)
    a_u, a_v = a2a(a_u, "y"), a2a(a_v, "z")
    a_u = a_u.astype(F32).sum(0).astype(BF).reshape(n_ph, mine, hidden)
    a_v = a_v.astype(F32).sum(0).astype(BF).reshape(n_ph, mine, hidden)
    both = a2a(jnp.concatenate([a_u, a_v], 2), ("p", "h"))
    both = both.reshape(2, n_ph // 2, mine, 2 * hidden).astype(F32).sum(1)

    pre0, up0 = both[0, :, hidden:], both[0, :, :hidden]
    pre1, up1 = both[1, :, :hidden], both[1, :, hidden:]
    act0 = silu_bf(pre0)
    pre1 = pre1 + dot(act0, m_all)
    act1 = silu_bf(pre1)
    slope1 = slope_bf(up1, pre1)
    up0 = up0 + dot_t1(slope1, m_all)
    slope0 = slope_bf(up0, pre0)

    to_first = jnp.stack([slope0, act0, slope1])
    to_last = jnp.stack([act1, slope1, act0])
    out = jnp.stack([to_first] * (n_ph // 2) + [to_last] * (n_ph // 2))
    out = a2a(out, ("p", "h")).transpose(1, 0, 2, 3).reshape(3, half, hidden)
    r = lax.all_gather(out[:1], "z", axis=1)
    pq = lax.all_gather(out[1:], "y", axis=1)
    rpq = jnp.concatenate([r, pq], 0)
    rpq = lax.all_gather(rpq, "c", axis=2).reshape(3, nz * tok, hidden)
    r, p, q = rpq[0], rpq[1], rpq[2]

    g_v = dot_t0(v, r).astype(BF)
    g_v = lax.psum_scatter(g_v, "y", scatter_dimension=0, tiled=True).astype(F32)
    u = (u.astype(F32) + dot_t1(q, w_3)).astype(BF)
    g_u = a2a(dot_t0(u, p).astype(BF), "z")
    g_u = g_u.reshape(nz, own, hidden).astype(F32).sum(0)

    squares = jnp.sum(g_u * g_u) + jnp.sum(g_v * g_v)
    grad_norm = jnp.sqrt(lax.psum(squares, AXES))
    factor = jnp.minimum(1.0, CLIP_NORM / grad_norm)
    g_in = jnp.where(first, g_v, g_u) * factor
    g_out = jnp.where(first, g_u, g_v) * factor
    return (g_in[None], g_out.T[None], grad_norm)


def solution(mesh):
    split = Mesh(mesh.devices.reshape(mesh.shape["pipe"], 2, 2, 4, 4), AXES)
    tensor, dp, all_model = ("h", "c"), ("z", "y"), ("h", "c", "z", "y")
    placed = (
        P(None, dp, tensor),
        P("p", all_model, None),
        P("p", None, all_model),
        P(None, dp, tensor),
    )
    return jax.shard_map(
        on_device,
        mesh=split,
        in_specs=placed,
        out_specs=(P("p", all_model, None), P("p", None, all_model), P()),
        check_vma=False,
    )
```

time: 890 us -> 433 us (0.49)
  waiting for transfers between devices: 597 us -> 163 us
  blocking collectives: 35.5 us -> 128 us
  matrix products: 90.1 us -> 29.6 us
  other arithmetic: 62.4 us -> 21.2 us
  local copies, waits for them, and re-layouts: 66.9 us -> 36.6 us
  starting transfers between devices: 15 us -> 34.9 us
    reduce_scatter x2 -> x1, waiting for transfers between devices: 208 us -> 0.01 us  [on_device(): lax.psum_scatter(g_v, 'y', scatter_dimension=0, tiled=True).astype(F32)]
    all_gather x7, waiting for transfers between devices: 288 us -> 109 us  [the longest x1 33.1 us: on_device(): pq = lax.all_gather(out[1:], 'y', axis=1)]
    ppermute x6 -> x1, waiting for transfers between devices: 100 us -> 12.1 us  [on_device(): w_3 = lax.ppermute(w_u, 'p', [(0, 1), (1, 0)])]
    dot_general x12 -> x7, matrix products: 90.1 us -> 29.6 us  [the longest x3 17.6 us: dot_t0(): lax.dot_general(a, b, (((0,), (0,)), ((), ())), preferred_element_type=F32)]
    all_to_all x0 -> x3, blocking collectives: none -> 55.7 us  [a2a(): return lax.all_to_all(value, axes, 0, 0, tiled=True)]
    all_to_all x0 -> x7, waiting for transfers between devices: none -> 41.4 us  [a2a(): return lax.all_to_all(value, axes, 0, 0, tiled=True)]
    all_to_all x0 -> x7, starting transfers between devices: none -> 32.8 us  [a2a(): return lax.all_to_all(value, axes, 0, 0, tiled=True)]
    reduce_sum x10 -> x9, other arithmetic: 40.5 us -> 8.77 us  [the longest x1 3.33 us: on_device(): a_v = a_v.astype(F32).sum(0).astype(BF)]
  transfers between devices with their start and end apart: 15 -> 16, of which waited for: 15 -> 10; matrix products, arithmetic and copies ran while one was open for 7% -> 12% of each run, Pallas kernels for 0% -> 0%
where the time goes in v1:
time: 433 us; the launch traced here: 431 us
  waiting for transfers between devices  163 us (38%)
  blocking collectives  128 us (30%)
  local copies, waits for them, and re-layouts  36.6 us (8%)
  starting transfers between devices  34.9 us (8%)
  matrix products  29.6 us (7%)
  other arithmetic  21.2 us (5%)
  between operations  17.5 us (4%)
    psum x1, blocking collectives, on_device(): grad_norm = jnp.sqrt(lax.psum(squares, AXES))  64.5 us
    all_to_all x3, blocking collectives, a2a(): return lax.all_to_all(value, axes, 0, 0, tiled=True)  55.7 us
    all_to_all x7, waiting for transfers between devices, a2a(): return lax.all_to_all(value, axes, 0, 0, tiled=True)  41.4 us
    all_gather x1, waiting for transfers between devices, on_device(): pq = lax.all_gather(out[1:], 'y', axis=1)  33.1 us
    all_to_all x7, starting transfers between devices, a2a(): return lax.all_to_all(value, axes, 0, 0, tiled=True)  32.8 us
    all_gather x1, waiting for transfers between devices, on_device(): w_3 = lax.all_gather(w_3, 'z', axis=0, tiled=True)  32.6 us
    all_gather x1, waiting for transfers between devices, on_device(): r = lax.all_gather(out[:1], 'z', axis=1)  20.2 us
    all_gather x1, waiting for transfers between devices, on_device(): rpq = lax.all_gather(rpq, 'c', axis=2).reshape(3, nz * tok, hidden)  19.5 us
  transfers between devices with their start and end apart: 16, of which 10 were waited for; matrix products, arithmetic and copies ran while one was open for 12% of the time, Pallas kernels for 0%

profile of v1, /device:TPU:0, one launch (start us, length us, event | category | flops | bytes accessed | tf_op | source)
XLA Modules:
  0.0 430.6 jit_solution(9673179844695942069)
XLA Ops:
  7.2 1.2 copy.33
  8.5 2.2 bitcast_select_fusion.1
  10.8 1.7 collective-permute-start
  12.5 12.1 %collective-permute-done = bf16[256,1024]{1,0:T(8,128)(2,1)S(1)} collective-permute-done((bf16[256,1024]{1,0:T(8,128)(2,1)}, bf16[256,1024]{1,0:T(8,128)(2,1)S(1)}, u32[]{:S(2)}, u32[]{:S(2)}) %collective-permute-start) | collective-permute-done | bytes 524320 | tf_op jit(solution)/shard_map/ppermute | solution.py:55
  26.2 3.8 broadcast_select_fusion
  30.0 3.3 select_n.60
  33.4 2.8 copy.31
  36.1 4.8 %all-to-all-start.1 = ((bf16[4,256,1024]{1,2,0:T(8,128)(2,1)}), bf16[4,256,1024]{1,2,0:T(8,128)(2,1)S(1)}, u32[]{:S(2)}, u32[]{:S(2)}) async-start(bf16[4,256,1024]{1,2,0:T(8,128)(2,1)} %bitcast.106), calls=%async_computation.1 | async-start | bytes 4194304 | tf_op jit(solution)/shard_map/all_to_all | solution.py:26
  40.9 3.5 all-gather.9.cloned.1.call-done
  44.4 32.6 %all-gather.13.cloned.1.call-done = bf16[1024,1024]{1,0:T(8,128)(2,1)} async-done(((bf16[256,1024]{1,0:T(8,128)(2,1)}), bf16[1024,1024]{1,0:T(8,128)(2,1)}) %all-gather.13.cloned.1.call-update) | async-done | bytes 2097168 | tf_op jit(solution)/shard_map/all_gather | solution.py:58
  76.9 3.5 fusion.5
  80.4 6.8 %all-to-all-start.7 = ((bf16[16,16,1024]{2,1,0:T(8,128)(2,1)}), bf16[16,16,1024]{2,1,0:T(8,128)(2,1)S(1)}, u32[]{:S(2)}, u32[]{:S(2)}) async-start(bf16[16,16,1024]{2,1,0:T(8,128)(2,1)} %bitcast.20), calls=%async_computation.7 | async-start | bytes 1048576 | tf_op jit(solution)/shard_map/all_to_all | solution.py:26
  87.3 4.6 %select_n.58 = bf16[256,4,4,256]{3,2,1,0:T(4,128)(2,1)} reshape(bf16[2,128,4096]{2,1,0:T(8,128)(2,1)} %get-tuple-element.22) | data formatting | bytes 4194304 | tf_op jit(solution)/shard_map/jit(_where)/select_n | solution.py:63
  91.8 3.6 copy.44
  95.5 4.5 %all_to_all.46 = bf16[4,256,1024]{2,1,0:T(8,128)(2,1)} reshape(bf16[4,256,4,256]{3,2,1,0:T(4,128)(2,1)} %bitcast.110) | data formatting | bytes 4194304 | tf_op jit(solution)/shard_map/all_to_all | solution.py:26
  100.0 4.5 %all-to-all-start = ((bf16[4,256,1024]{2,1,0:T(8,128)(2,1)}), bf16[4,256,1024]{2,1,0:T(8,128)(2,1)}, u32[]{:S(2)}, u32[]{:S(2)}) async-start(bf16[4,256,1024]{2,1,0:T(8,128)(2,1)} %all_to_all.46), calls=%async_computation | async-start | bytes 4194304 | tf_op jit(solution)/shard_map/all_to_all | solution.py:26
  104.6 7.4 %all_gather.36 = bf16[64,1024]{1,0:T(8,128)(2,1)} all-gather(bf16[16,1024]{1,0:T(8,128)(2,1)S(1)} %reduce_sum.101), channel_id=1, replica_groups=mesh['p'=2,'h'=2,'c'=2,'z'=4,'y'=4] {'h','c'}, dimensions={0}, use_global_device_ids=true | all-gather | bytes 163840 | tf_op jit(solution)/shard_map/all_gather | solution.py:73
  112.0 2.5 copy.32
  114.5 4.6 %convolution_convert_fusion.2 = bf16[1024,1024]{1,0:T(8,128)(2,1)S(1)} fusion(bf16[1024,1024]{1,0:T(8,128)(2,1)} %bitcast.113, bf16[1024,1024]{1,0:T(8,128)(2,1)} %all-gather.9.cloned.1.call-done), kind=kOutput, calls=%fused_computation.15 | convolution fusion | flops 2148532224 | bytes 6291456 | tf_op jit(solution)/shard_map/dot_general | solution.py:14
  119.1 1.5 copy.43
  120.6 11.8 %all-to-all-done = bf16[4,256,1024]{2,1,0:T(8,128)(2,1)} async-done(((bf16[4,256,1024]{2,1,0:T(8,128)(2,1)}), bf16[4,256,1024]{2,1,0:T(8,128)(2,1)}, u32[]{:S(2)}, u32[]{:S(2)}) %all-to-all-start) | async-done | bytes 2097184 | tf_op jit(solution)/shard_map/all_to_all | solution.py:26
  132.4 3.8 all-to-all-start.2
  136.2 4.6 %convolution_convert_fusion.1 = bf16[1024,1024]{1,0:T(8,128)(2,1)S(1)} fusion(bf16[1024,1024]{1,0:T(8,128)(2,1)} %bitcast.1, bf16[1024,1024]{1,0:T(8,128)(2,1)} %all-gather.11.cloned.1.call-done), kind=kOutput, calls=%fused_computation.14 | convolution fusion | flops 2148532224 | bytes 6291456 | tf_op jit(solution)/shard_map/dot_general | solution.py:14
  140.7 1.5 copy.42
  142.3 4.8 %all-to-all-start.4 = ((bf16[2,4,128,1024]{3,2,1,0:T(8,128)(2,1)}), bf16[2,4,128,1024]{3,2,1,0:T(8,128)(2,1)}, u32[]{:S(2)}, u32[]{:S(2)}) async-start(bf16[2,4,128,1024]{3,2,1,0:T(8,128)(2,1)} %bitcast.108), calls=%async_computation.4 | async-start | bytes 4194304 | tf_op jit(solution)/shard_map/all_to_all | solution.py:26
  147.1 1.7 reduce_sum.96
  148.8 1.3 all-to-all-done.4
  150.1 4.7 %all-to-all-start.3 = ((bf16[4,128,1024]{2,1,0:T(8,128)(2,1)}), bf16[4,128,1024]{2,1,0:T(8,128)(2,1)S(1)}, u32[]{:S(2)}, u32[]{:S(2)}) async-start(bf16[4,128,1024]{2,1,0:T(8,128)(2,1)} %reduce_sum.96), calls=%async_computation.3 | async-start | bytes 2097152 | tf_op jit(solution)/shard_map/all_to_all | solution.py:26
  154.8 3.3 reduce_sum.98
  158.1 13.5 %all-to-all-done.3 = bf16[4,128,1024]{2,1,0:T(8,128)(2,1)S(1)} async-done(((bf16[4,128,1024]{2,1,0:T(8,128)(2,1)}), bf16[4,128,1024]{2,1,0:T(8,128)(2,1)S(1)}, u32[]{:S(2)}, u32[]{:S(2)}) %all-to-all-start.3) | async-done | bytes 1048608 | tf_op jit(solution)/shard_map/all_to_all | solution.py:26
  171.6 3.5 all-to-all-start.5
  175.4 14.9 %all-to-all-done.5 = bf16[4,128,1024]{2,1,0:T(8,128)(2,1)S(1)} async-done(((bf16[4,128,1024]{2,1,0:T(8,128)(2,1)}), bf16[4,128,1024]{2,1,0:T(8,128)(2,1)S(1)}, u32[]{:S(2)}, u32[]{:S(2)}) %all-to-all-start.5) | async-done | bytes 1048608 | tf_op jit(solution)/shard_map/all_to_all | solution.py:26
  190.5 12.1 %all_to_all.72 = bf16[4,32,2048]{2,1,0:T(8,128)(2,1)S(1)} all-to-all(bf16[4,32,2048]{2,1,0:T(8,128)(2,1)S(1)} %pad_maximum_fusion.2), channel_id=1, replica_groups=mesh['p'=2,'h'=2,'c'=2,'z'=4,'y'=4] {'p','h'}, dimensions={0} | all-to-all | bytes 1048576 | tf_op jit(solution)/shard_map/all_to_all | solution.py:26
  202.8 2.2 fusion.31
  205.9 12.3 %all_to_all.73 = bf16[4,3,32,1024]{3,2,1,0:T(8,128)(2,1)S(1)} all-to-all(bf16[4,3,32,1024]{3,2,1,0:T(8,128)(2,1)S(1)} %pad_maximum_fusion.1), channel_id=1, replica_groups=mesh['p'=2,'h'=2,'c'=2,'z'=4,'y'=4] {'p','h'}, dimensions={0} | all-to-all | bytes 1572864 | tf_op jit(solution)/shard_map/all_to_all | solution.py:26
  220.0 20.2 %all-gather.17.cloned.1.call-done = bf16[1,4,128,1024]{3,2,0,1:T(8,128)(2,1)} async-done(((bf16[1,1,128,1024]{3,2,0,1:T(8,128)(2,1)}), bf16[1,4,128,1024]{3,2,0,1:T(8,128)(2,1)}) %all-gather.17.cloned.1.call-update) | async-done | bytes 1048592 | tf_op jit(solution)/shard_map/all_gather | solution.py:100
  240.2 33.1 %all-gather.19.cloned.1.call-done = bf16[2,4,128,1024]{3,2,0,1:T(8,128)(2,1)} async-done(((bf16[2,1,128,1024]{3,2,0,1:T(8,128)(2,1)}), bf16[2,4,128,1024]{3,2,0,1:T(8,128)(2,1)}) %all-gather.19.cloned.1.call-update) | async-done | bytes 2097168 | tf_op jit(solution)/shard_map/all_gather | solution.py:101
  273.3 3.8 pad_maximum_fusion
  277.2 19.5 %all-gather.21.cloned.1.call-done = bf16[3,4,256,1024]{3,2,0,1:T(8,128)(2,1)} async-done(((bf16[3,4,128,1024]{3,2,0,1:T(8,128)(2,1)}), bf16[3,4,256,1024]{3,2,0,1:T(8,128)(2,1)}) %all-gather.21.cloned.1.call-update) | async-done | bytes 6291472 | tf_op jit(solution)/shard_map/all_gather | solution.py:103
  296.7 5.6 %fusion.34 = (bf16[1,4,256,1024]{3,2,0,1:T(8,128)(2,1)S(1)}, bf16[1,4,256,1024]{3,2,0,1:T(8,128)(2,1)}, bf16[1,4,256,1024]{3,2,0,1:T(8,128)(2,1)}) fusion(bf16[3,4,256,1024]{3,2,0,1:T(8,128)(2,1)} %all-gather.21.cloned.1.call-done), kind=kLoop, calls=%fused_computation.64 | loop fusion | bytes 12582912 | tf_op jit(solution)/shard_map/slice | solution.py:104
  302.3 5.3 %convolution_convert_fusion = bf16[1024,1024]{1,0:T(8,128)(2,1)} fusion(bf16[1024,1024]{1,0:T(8,128)(2,1)} %bitcast.1, bf16[1024,1024]{1,0:T(8,128)(2,1)S(1)} %bitcast.121), kind=kOutput, calls=%fused_computation.13 | convolution fusion | flops 2148532224 | bytes 6291456 | tf_op jit(solution)/shard_map/dot_general | solution.py:18
  307.6 1.6 copy-done.1
  309.2 8.8 %fusion.4 = bf16[1024,1024]{1,0:T(8,128)(2,1)} fusion(bf16[1024,1024]{1,0:T(8,128)(2,1)} %bitcast.120, bf16[1024,1024]{1,0:T(8,128)(2,1)S(1)} %bitcast.114, bf16[1024,1024]{1,0:T(8,128)(2,1)} %bitcast.119, bf16[1024,1024]{1,0:T(8,128)(2,1)} %all-gather.13.cloned.1.call-done), kind=kOutput, calls=%fused_computation.12 | convolution fusion | flops 4299161600 | bytes 10485760 | tf_op jit(solution)/shard_map/dot_general | solution.py:18
  318.0 31.3 %all_to_all.74 = bf16[4,256,1024]{2,1,0:T(8,128)(2,1)S(1)} all-to-all(bf16[4,256,1024]{2,1,0:T(8,128)(2,1)} %bitcast.115), channel_id=1, replica_groups=mesh['p'=2,'h'=2,'c'=2,'z'=4,'y'=4] {'z'}, dimensions={0} | all-to-all | bytes 4194304 | tf_op jit(solution)/shard_map/all_to_all | solution.py:26
  350.5 1.9 fusion.16
  353.7 64.5 %psum.7 = f32[]{:T(128)} all-reduce(f32[]{:T(128)S(6)} %add.46), channel_id=1, replica_groups=mesh['p'=2,'h'=2,'c'=2,'z'=4,'y'=4] {'p','h','c','z','y'}, use_global_device_ids=true, to_apply=%region_10.11 | all-reduce | flops 1 | bytes 8 | tf_op jit(solution)/shard_map/psum | solution.py:113
  419.0 2.3 fusion.18
  421.3 1.3 copy.38
  (43 shorter events, 6.4 us)
Async XLA Ops:
  7.2 37.2 %all-gather.9.cloned.1.call-start = ((), (), s32[]{:S(2)}) async-start(), calls=%async_computation.11 | async-start | bytes 2621440 | tf_op jit(solution)/shard_map/all_gather | solution.py:56
  8.5 17.7 %copy-start.2 = (bf16[2,128,4096]{2,1,0:T(8,128)(2,1)S(1)}, bf16[2,128,4096]{2,1,0:T(8,128)(2,1)}, u32[]{:S(2)}) copy-start(bf16[2,128,4096]{2,1,0:T(8,128)(2,1)} %param.7) | copy-start | bytes 6291460
  10.7 66.2 %all-gather.13.cloned.1.call-start = ((), (), s32[]{:S(2)}) async-start(), calls=%async_computation.13 | async-start | bytes 2621440 | tf_op jit(solution)/shard_map/all_gather | solution.py:58
  10.8 13.8 %collective-permute-start = (bf16[256,1024]{1,0:T(8,128)(2,1)}, bf16[256,1024]{1,0:T(8,128)(2,1)S(1)}, u32[]{:S(2)}, u32[]{:S(2)}) collective-permute-start(bf16[256,1024]{1,0:T(8,128)(2,1)} %get-tuple-element.25), channel_id=1, source_target_pairs={{0,64},{64,0},{1,65},{65,1},{2,66},{66,2},{3,67},{67,3},{4,68},{68... | collective-permute-start | bytes 1572872 | tf_op jit(solution)/shard_map/ppermute | solution.py:55
  24.6 0.8 copy-start.3
  25.4 110.7 %all-gather.11.cloned.1.call-start = ((), (), s32[]{:S(2)}) async-start(), calls=%async_computation.12 | async-start | bytes 2621440 | tf_op jit(solution)/shard_map/all_gather | solution.py:57
  36.1 44.3 %all-to-all-start.1 = ((bf16[4,256,1024]{1,2,0:T(8,128)(2,1)}), bf16[4,256,1024]{1,2,0:T(8,128)(2,1)S(1)}, u32[]{:S(2)}, u32[]{:S(2)}) async-start(bf16[4,256,1024]{1,2,0:T(8,128)(2,1)} %bitcast.106), calls=%async_computation.1 | async-start | bytes 4194304 | tf_op jit(solution)/shard_map/all_to_all | solution.py:26
  80.4 19.5 %all-to-all-start.7 = ((bf16[16,16,1024]{2,1,0:T(8,128)(2,1)}), bf16[16,16,1024]{2,1,0:T(8,128)(2,1)S(1)}, u32[]{:S(2)}, u32[]{:S(2)}) async-start(bf16[16,16,1024]{2,1,0:T(8,128)(2,1)} %bitcast.20), calls=%async_computation.7 | async-start | bytes 1048576 | tf_op jit(solution)/shard_map/all_to_all | solution.py:26
  100.0 32.4 %all-to-all-start = ((bf16[4,256,1024]{2,1,0:T(8,128)(2,1)}), bf16[4,256,1024]{2,1,0:T(8,128)(2,1)}, u32[]{:S(2)}, u32[]{:S(2)}) async-start(bf16[4,256,1024]{2,1,0:T(8,128)(2,1)} %all_to_all.46), calls=%async_computation | async-start | bytes 4194304 | tf_op jit(solution)/shard_map/all_to_all | solution.py:26
  104.5 98.3 %all-gather.15.cloned.1.call-start = ((), (), s32[]{:S(2)}) async-start(), calls=%async_computation.14 | async-start | bytes 2228224 | tf_op jit(solution)/shard_map/all_gather | solution.py:74
  132.4 9.9 %all-to-all-start.2 = ((bf16[2,4,128,1024]{3,2,1,0:T(8,128)(2,1)}), bf16[2,4,128,1024]{3,2,1,0:T(8,128)(2,1)S(1)}, u32[]{:S(2)}, u32[]{:S(2)}) async-start(bf16[2,4,128,1024]{3,2,1,0:T(8,128)(2,1)} %bitcast.107), calls=%async_computation.2 | async-start | bytes 4194304 | tf_op jit(solution)/shard_map/all_to_all | solution.py:26
  142.3 7.8 %all-to-all-start.4 = ((bf16[2,4,128,1024]{3,2,1,0:T(8,128)(2,1)}), bf16[2,4,128,1024]{3,2,1,0:T(8,128)(2,1)}, u32[]{:S(2)}, u32[]{:S(2)}) async-start(bf16[2,4,128,1024]{3,2,1,0:T(8,128)(2,1)} %bitcast.108), calls=%async_computation.4 | async-start | bytes 4194304 | tf_op jit(solution)/shard_map/all_to_all | solution.py:26
  150.1 21.5 %all-to-all-start.3 = ((bf16[4,128,1024]{2,1,0:T(8,128)(2,1)}), bf16[4,128,1024]{2,1,0:T(8,128)(2,1)S(1)}, u32[]{:S(2)}, u32[]{:S(2)}) async-start(bf16[4,128,1024]{2,1,0:T(8,128)(2,1)} %reduce_sum.96), calls=%async_computation.3 | async-start | bytes 2097152 | tf_op jit(solution)/shard_map/all_to_all | solution.py:26
  171.6 18.6 %all-to-all-start.5 = ((bf16[4,128,1024]{2,1,0:T(8,128)(2,1)}), bf16[4,128,1024]{2,1,0:T(8,128)(2,1)S(1)}, u32[]{:S(2)}, u32[]{:S(2)}) async-start(bf16[4,128,1024]{2,1,0:T(8,128)(2,1)} %reduce_sum.98), calls=%async_computation.5 | async-start | bytes 2097152 | tf_op jit(solution)/shard_map/all_to_all | solution.py:26
  175.1 65.0 %all-gather.17.cloned.1.call-start = ((), (), s32[]{:S(2)}) async-start(), calls=%async_computation.15 | async-start | bytes 1310720 | tf_op jit(solution)/shard_map/all_gather | solution.py:100
  202.8 2.2 copy-start
  219.0 54.3 %all-gather.19.cloned.1.call-start = ((), (), s32[]{:S(2)}) async-start(), calls=%async_computation.16 | async-start | bytes 2621440 | tf_op jit(solution)/shard_map/all_gather | solution.py:101
  219.9 76.8 %all-gather.21.cloned.1.call-start = ((), (), s32[]{:S(2)}) async-start(), calls=%async_computation.18 | async-start | bytes 9437184 | tf_op jit(solution)/shard_map/all_gather | solution.py:103
  277.1 73.4 %reduce-scatter.2.cloned.1.call-start = ((), (), s32[]{:S(2)}) async-start(), calls=%async_computation.17 | async-start | bytes 2621440 | tf_op jit(solution)/shard_map/reduce_scatter | solution.py:107
  307.6 1.6 copy-start.1
Sparse Core Ops, SparseCore 0:
  10.9 33.4 all-gather.8
  46.0 30.8 all-gather.12
  79.2 35.1 all-gather.10
  116.4 46.4 all-gather.14
  219.1 21.0 all-gather.16
  242.2 30.9 all-gather.18
  277.2 19.4 all-gather.20
  307.8 31.0 reduce-scatter.1
